TPU v7x, 256 devices: a whole 4x4x8 slice. The times are simulated.
256 devices in a mesh: outer: 16 (over z_lo, x), inner: 16 (over y, z_hi, core).
Axes of the slice: x: 4, y: 4, z: 8 (z_hi: 2, z_lo: 4; z = z_hi * 4 + z_lo), core: 2. Of those that a mesh axis runs over, the one named last changes fastest.
Arguments:
- queries: bfloat16 [8192, 2, 4096], P('outer', None, 'inner'), may hold values from -52 to 52
- keys: bfloat16 [8192, 2, 4096], P('outer', None, 'inner'), may hold values from -6 to 6
- values: bfloat16 [8192, 2, 4096], P('outer', None, 'inner'), may hold values from -6 to 6
Outputs:
- attended: bfloat16 [8192, 2, 4096], P(('outer', 'inner'))
All inputs are finite; a program needn't handle non-finite values.
Results may differ from a plain program's by a relative error of at most 0.004.
Values may be sent and summed in bfloat16 or wider, within the bound.
A program may use at most 128 MiB of HBM per device.

v0:
```python
from functools import partial
import math

import jax
import jax.numpy as jnp
from jax import lax
from jax.sharding import PartitionSpec as P

HEAD_DIM = 128


def attend_keys(running, key_block, value_block, query_heads, head_count):
    peak_rows, totals, numerator = running
    key_count = key_block.shape[0]
    key_heads = key_block.reshape(key_count, head_count, HEAD_DIM)
    value_heads = value_block.reshape(key_count, head_count, HEAD_DIM)
    scores = jnp.einsum(
        "qhd,khd->qhk", query_heads, key_heads, preferred_element_type=jnp.float32
    ) * (1.0 / math.sqrt(HEAD_DIM))
    new_peaks = jnp.maximum(peak_rows, jnp.max(scores, axis=2))
    shrink = jnp.exp(peak_rows - new_peaks)
    weights = jnp.exp(scores - new_peaks[..., None])
    totals = totals * shrink + jnp.sum(weights, axis=2)
    numerator = numerator * shrink[..., None] + jnp.einsum(
        "qhk,khd->qhd",
        weights.astype(jnp.bfloat16),
        value_heads,
        preferred_element_type=jnp.float32,
    )
    return (new_peaks, totals, numerator)


def attend_piece(running, pieces, start_row, query_part, head_count):
    key_rows, value_rows = pieces
    row_count = query_part.shape[0]
    query_heads = query_part.reshape(row_count, head_count, HEAD_DIM)
    block_count = key_rows.shape[0] // row_count
    key_blocks = key_rows.reshape(block_count, row_count, key_rows.shape[1])
    value_blocks = value_rows.reshape(block_count, row_count, value_rows.shape[1])

    def one_block(state, blocks):
        return (attend_keys(state, blocks[0], blocks[1], query_heads, head_count), None)

    running, unused = lax.scan(one_block, running, (key_blocks, value_blocks))
    return running


def start_state(row_count, head_count):
    peak_rows = jnp.full((row_count, head_count), -1e30, jnp.float32)
    totals = jnp.zeros((row_count, head_count), jnp.float32)
    numerator = jnp.zeros((row_count, head_count, HEAD_DIM), jnp.float32)
    return (peak_rows, totals, numerator)


def finish_state(running):
    peak_rows, totals, numerator = running
    averaged = numerator / totals[..., None]
    return averaged.reshape(numerator.shape[0], -1).astype(jnp.bfloat16)


def flatten(array):
    return array.reshape(array.shape[0], array.shape[1] * array.shape[2])


def per_device(queries, keys, values):
    tok_rows, networks, local_cols = queries.shape
    flat_queries, flat_keys, flat_values = (flatten(queries), flatten(keys), flatten(values))
    head_count = networks * local_cols // HEAD_DIM
    folder = partial(attend_piece, query_part=flat_queries, head_count=head_count)
    running = folder(
        start_state(tok_rows, head_count),
        (
            lax.all_gather(flat_keys, "outer", axis=0, tiled=True),
            lax.all_gather(flat_values, "outer", axis=0, tiled=True),
        ),
        jnp.int32(0),
    )
    local_out = finish_state(running).reshape(tok_rows, networks, local_cols)
    attended = lax.all_to_all(local_out, "inner", split_axis=0, concat_axis=2, tiled=True)
    return attended


def solution(mesh):
    return jax.shard_map(
        per_device,
        mesh=mesh,
        in_specs=(P("outer", None, "inner"), P("outer", None, "inner"), P("outer", None, "inner")),
        out_specs=P(("outer", "inner"), None, None),
        check_vma=False,
    )
```

profile of v0, /device:TPU:1, one launch (start us, length us, event | category | flops | bytes accessed | tf_op | source)
XLA Modules:
  0.0 317.8 jit_solution(2837683536750189921)
XLA Ops:
  6.5 1.9 copy.35
  8.5 1.9 copy.36
  10.5 1.3 copy.21
  12.1 103.0 %all-gather.3.cloned.1.call-done = bf16[8192,512]{1,0:T(8,128)(2,1)} async-done(((bf16[512,512]{1,0:T(8,128)(2,1)}), bf16[8192,512]{1,0:T(8,128)(2,1)}) %all-gather.3.cloned.1.call-update) | async-done | bytes 8388624 | tf_op jit(solution)/shard_map/all_gather | solution.py:73
  115.1 101.0 %all-gather.5.cloned.1.call-done = bf16[8192,512]{1,0:T(8,128)(2,1)} async-done(((bf16[512,512]{1,0:T(8,128)(2,1)}), bf16[8192,512]{1,0:T(8,128)(2,1)}) %all-gather.5.cloned.1.call-update) | async-done | bytes 8388624 | tf_op jit(solution)/shard_map/all_gather | solution.py:74
  216.1 70.4 %while.15 = (s32[]{:T(128)}, f32[512,4]{0,1:T(4,128)S(1)}, f32[512,4]{0,1:T(4,128)S(1)}, f32[512,4,128]{0,2,1:T(8,128)S(1)}, bf16[16,512,512]{2,1,0:T(8,128)(2,1...) while((s32[]{:T(128)}, f32[512,4]{0,1:T(4,128)S(1)}, ...), condition=%wide.region_3.4_spmd.clone, body=%wide.region_0.3_spmd.clone.sunk | while | flops 546056192 | bytes 20578420 | solution.py:44
  216.1 1.3 constant_dynamic-slice_fusion.3
  217.8 0.8 bitcast_reduce_fusion.2
  218.6 0.7 fusion.29
  219.3 1.1 fusion.31
  220.5 1.3 constant_dynamic-slice_fusion.3
  222.2 0.8 bitcast_reduce_fusion.2
  223.0 0.7 fusion.29
  223.7 1.1 fusion.31
  224.9 1.3 constant_dynamic-slice_fusion.3
  226.6 0.8 bitcast_reduce_fusion.2
  228.1 1.1 fusion.31
  229.3 1.3 constant_dynamic-slice_fusion.3
  231.0 0.8 bitcast_reduce_fusion.2
  231.8 0.7 fusion.29
  232.5 1.1 fusion.31
  233.7 1.3 constant_dynamic-slice_fusion.3
  235.4 0.8 bitcast_reduce_fusion.2
  236.9 1.1 fusion.31
  238.1 1.3 constant_dynamic-slice_fusion.3
  239.8 0.8 bitcast_reduce_fusion.2
  240.6 0.7 fusion.29
  241.3 1.1 fusion.31
  242.5 1.3 constant_dynamic-slice_fusion.3
  244.2 0.8 bitcast_reduce_fusion.2
  245.8 1.1 fusion.31
  246.9 1.3 constant_dynamic-slice_fusion.3
  248.6 0.8 bitcast_reduce_fusion.2
  249.4 0.7 fusion.29
  250.2 1.1 fusion.31
  251.3 1.3 constant_dynamic-slice_fusion.3
  253.0 0.8 bitcast_reduce_fusion.2
  253.8 0.7 fusion.29
  254.6 1.1 fusion.31
  255.7 1.3 constant_dynamic-slice_fusion.3
  257.4 0.8 bitcast_reduce_fusion.2
  258.2 0.7 fusion.29
  259.0 1.1 fusion.31
  260.1 1.3 constant_dynamic-slice_fusion.3
  261.9 0.8 bitcast_reduce_fusion.2
  262.6 0.7 fusion.29
  263.4 1.1 fusion.31
  264.5 1.3 constant_dynamic-slice_fusion.3
  266.3 0.8 bitcast_reduce_fusion.2
  267.8 1.1 fusion.31
  268.9 1.3 constant_dynamic-slice_fusion.3
  270.7 0.8 bitcast_reduce_fusion.2
  272.2 1.1 fusion.31
  273.4 1.3 constant_dynamic-slice_fusion.3
  275.1 0.8 bitcast_reduce_fusion.2
  276.6 1.1 fusion.31
  277.8 1.3 constant_dynamic-slice_fusion.3
  279.5 0.8 bitcast_reduce_fusion.2
  281.0 1.1 fusion.31
  282.2 1.3 constant_dynamic-slice_fusion.3
  283.9 0.8 bitcast_reduce_fusion.2
  285.4 1.1 fusion.31
  287.2 22.5 %all_to_all.18 = bf16[512,2,256]{2,1,0:T(2,128)(2,1)S(1)} all-to-all(bf16[512,2,256]{2,1,0:T(2,128)(2,1)S(1)} %copy.25), channel_id=1, replica_groups=mesh['outer'=16,'inner'=16] {'inner'}, dimensions={0} | all-to-all | bytes 1048576 | tf_op jit(solution)/shard_map/all_to_all | solution.py:79
  310.0 0.9 reshape.33
  (100 shorter events, 14.3 us)
Async XLA Ops:
  6.5 108.6 %all-gather.3.cloned.1.call-start = ((), (), s32[]{:S(2)}) async-start(), calls=%async_computation.1 | async-start | bytes 8912896 | tf_op jit(solution)/shard_map/all_gather | solution.py:73
  8.5 207.6 %all-gather.5.cloned.1.call-start = ((), (), s32[]{:S(2)}) async-start(), calls=%async_computation.2 | async-start | bytes 8912896 | tf_op jit(solution)/shard_map/all_gather | solution.py:74
Sparse Core Ops, SparseCore 0:
  9.1 105.9 all-gather.2
  116.9 99.1 all-gather.4
where the time goes:
time: 322 us; the launch traced here: 318 us
  waiting for transfers between devices  204 us (63%)
  local copies, waits for them, and re-layouts  34.4 us (11%)
  matrix products  30.6 us (10%)
  blocking collectives  22.5 us (7%)
  between operations  13.5 us (4%)
  other arithmetic  11.9 us (4%)
    all_gather x1, waiting for transfers between devices, per_device(): lax.all_gather(flat_keys, 'outer', axis=0, tiled=True)  103 us
    all_gather x1, waiting for transfers between devices, per_device(): lax.all_gather(flat_values, 'outer', axis=0, tiled=True)  101 us
    dynamic_slice x48, local copies, waits for them, and re-layouts, attend_piece(): running, unused = lax.scan(one_block, running, (key_blocks, value_blocks))  27.2 us
    all_to_all x1, blocking collectives, per_device(): lax.all_to_all(local_out, 'inner', split_axis=0, concat_axis=2, tiled=True)  22.5 us
    dot_general x16, matrix products, attend_keys(): jnp.einsum('qhk,khd->qhd', weights.astype(jnp.bfloat16), value_heads, pre...  18.3 us
    dot_general x16, matrix products, attend_keys(): jnp.einsum('qhd,khd->qhk', query_heads, key_heads, preferred_element_type...  12.4 us
    reduce_sum x16, other arithmetic, attend_keys(): totals = totals * shrink + jnp.sum(weights, axis=2)  11.3 us
  transfers between devices with their start and end apart: 2, of which 2 were waited for; matrix products, arithmetic and copies ran while one was open for 1% of the time, Pallas kernels for 0%

commit v1 on v0

v1 whole, which is shorter than its diff:
```python
import functools
import math

import jax
import jax.numpy as jnp
from jax import lax
from jax.experimental import pallas as pl
from jax.experimental.pallas import tpu as pltpu
from jax.sharding import PartitionSpec as P

HEAD_DIM = 128
XS = 4
ZS = 4
HALVES = 2
FACTOR = math.log2(math.e) / math.sqrt(HEAD_DIM)
MESH = pl.DeviceIdType.MESH


def kernel(
    ni, tok, q_ref, k_ref, v_ref, out_ref,
    qb, kvb, acc, peak, ob, obuf,
    zsend, zrecv, xsend, xrecv, osend, orecv,
):
    half = tok // HALVES
    rows_to = tok // ni
    bq = half
    outer, inner = lax.axis_index("outer"), lax.axis_index("inner")
    x, zl = outer % XS, outer // XS
    core, group = inner % 2, inner // 2
    right, left = (x + 1) % XS, (x + XS - 1) % XS

    def at(x_at, z_at, inner_at):
        return {"outer": z_at * XS + x_at, "inner": inner_at}

    barrier = pltpu.get_barrier_semaphore()

    def hello(index, carry):
        z_at, inner_at = index // ni, index % ni

        @pl.when(jnp.logical_or(z_at != zl, inner_at != inner))
        def _():
            pl.semaphore_signal(barrier, inc=1, device_id=at(x, z_at, inner_at), device_id_type=MESH)

        return carry

    lax.fori_loop(0, ZS * ni, hello, 0)
    for x_at in (left, right):
        pl.semaphore_signal(barrier, inc=1, device_id=at(x_at, zl, inner), device_id_type=MESH)

    acc[...] = jnp.zeros_like(acc)
    peak[...] = jnp.full_like(peak, -1e30)
    keeps = zl // 2 == core
    mine = zl % 2

    @pl.when(keeps)
    def _():
        qb[zl] = q_ref[core, mine]
        for h in range(HALVES):
            kvb[zl, h, x, 0] = k_ref[core, mine, h]
            kvb[zl, h, x, 1] = v_ref[core, mine, h]

    pl.semaphore_wait(barrier, ZS * ni - 1 + 2)

    def z_copy(piece, hh, net):
        z_at = 2 * core + hh
        if piece == 0:
            src, dst = q_ref.at[net, hh], qb.at[zl]
        else:
            h, kv = (piece - 1) // 2, (piece - 1) % 2
            src, dst = (k_ref, v_ref)[kv].at[net, hh, h], kvb.at[zl, h, x, kv]
        return pltpu.make_async_remote_copy(
            src_ref=src, dst_ref=dst,
            send_sem=zsend.at[piece, hh, net], recv_sem=zrecv.at[piece, zl],
            device_id=at(x, z_at, group * 2 + net), device_id_type=MESH,
        )

    def to_all(act):
        for piece in range(1 + 2 * HALVES):
            for hh in range(2):
                for net in range(2):
                    goes = jnp.logical_or(2 * core + hh != zl, net != core)

                    @pl.when(goes)
                    def _(piece=piece, hh=hh, net=net):
                        act(z_copy(piece, hh, net))

    to_all(lambda copy: copy.start())

    def z_of(j):
        flip = zl + 1 - 2 * (zl % 2)
        return ((zl if j % 2 == 0 else flip) + 2 * (j // 2)) % ZS

    def z_wait(piece, z_at):
        if piece == 0:
            ref = qb.at[z_at]
        else:
            h, kv = (piece - 1) // 2, (piece - 1) % 2
            ref = kvb.at[z_at, h, x, kv]
        pltpu.make_async_remote_copy(
            src_ref=ref, dst_ref=ref, send_sem=zsend.at[0, 0, 0], recv_sem=zrecv.at[piece, z_at],
            device_id=at(right, zl, inner), device_id_type=MESH,
        ).wait_recv()

    def z_arrived(piece, j):
        if j == 0:
            @pl.when(jnp.logical_not(keeps))
            def _():
                z_wait(piece, zl)
        else:
            z_wait(piece, z_of(j))

    def x_copy(kind, j, h):
        z_at = z_of(j)
        if kind < 2:
            ref = kvb.at[z_at, h, x]
        elif kind == 2:
            ref = kvb.at[z_at, h, left, 0]
        else:
            ref = kvb.at[z_at, h, right, 1]
        return pltpu.make_async_remote_copy(
            src_ref=ref, dst_ref=ref,
            send_sem=xsend.at[kind, j, h], recv_sem=xrecv.at[kind, j, h],
            device_id=at((right, left)[kind % 2], zl, inner), device_id_type=MESH,
        )

    def x_wait(kind, j, h):
        z_at = z_of(j)
        far = (x + 2) % XS
        ref = (kvb.at[z_at, h, left], kvb.at[z_at, h, right], kvb.at[z_at, h, far, 0], kvb.at[z_at, h, far, 1])[kind]
        pltpu.make_async_remote_copy(
            src_ref=ref, dst_ref=ref, send_sem=xsend.at[kind, j, h], recv_sem=xrecv.at[kind, j, h],
            device_id=at(right, zl, inner), device_id_type=MESH,
        ).wait_recv()

    def stage_a(t):
        j, h = t // HALVES, t % HALVES
        z_arrived(1 + 2 * h, j)
        z_arrived(2 + 2 * h, j)
        x_copy(0, j, h).start()
        x_copy(1, j, h).start()

    def stage_b(t):
        j, h = t // HALVES, t % HALVES
        x_wait(0, j, h)
        x_copy(2, j, h).start()
        x_wait(1, j, h)
        x_copy(3, j, h).start()

    def stage_c(t):
        j, h = t // HALVES, t % HALVES
        x_wait(2, j, h)
        x_wait(3, j, h)

    per = tok // bq

    def attend(t, block):
        j, h = t // HALVES, t % HALVES
        z_at = z_of(j)
        rows = pl.ds(pl.multiple_of(block * bq, bq), bq)
        q = qb[block // per, pl.ds(pl.multiple_of((block % per) * bq, bq), bq)]
        keys = kvb[z_at, h, :, 0].reshape(XS * half, HEAD_DIM)
        values = kvb[z_at, h, :, 1].reshape(XS * half, HEAD_DIM)
        scores = lax.dot_general(q, keys, (((1,), (1,)), ((), ())), preferred_element_type=jnp.float32)
        before = peak[rows]
        now = jnp.maximum(before, jnp.max(scores, axis=1, keepdims=True) * FACTOR)
        peak[rows] = now
        shrink = jnp.exp2(before - now)
        weights = jnp.exp2(scores * FACTOR - jnp.tile(now, (1, XS * half // HEAD_DIM)))
        wide = jnp.concatenate([values, jnp.ones_like(values)], axis=1)
        new = jnp.dot(weights.astype(jnp.bfloat16), wide, preferred_element_type=jnp.float32)
        total = acc[rows] * jnp.tile(shrink, (1, 2)) + new
        return rows, total

    def fold(t):
        def body(block, carry):
            rows, total = attend(t, block)
            acc[rows] = total
            return carry

        lax.fori_loop(0, ZS * per, body, 0)

    steps = ZS * HALVES
    dests = bq // rows_to

    def o_copies(block, act):
        z_at = block // per

        def one(index, carry):
            inner_at = (block % per) * dests + index

            @pl.when(jnp.logical_or(z_at != zl, inner_at != inner))
            def _():
                act(pltpu.make_async_remote_copy(
                    src_ref=ob.at[block * dests + index],
                    dst_ref=obuf.at[core * 2 * ni + group * 4 + zl],
                    send_sem=osend, recv_sem=orecv,
                    device_id=at(x, z_at, inner_at), device_id_type=MESH,
                ))

            return carry

        lax.fori_loop(0, dests, one, 0)

    stage_a(0)
    stage_a(1)
    stage_b(0)
    for j in range(ZS):
        z_arrived(0, j)
    for t in range(steps - 1):
        if t + 2 < steps:
            stage_a(t + 2)
        stage_b(t + 1)
        stage_c(t)
        fold(t)
    stage_c(steps - 1)

    def last(block, carry):
        rows, total = attend(steps - 1, block)
        done = (total[:, :HEAD_DIM] / total[:, HEAD_DIM:]).astype(jnp.bfloat16)
        ob[pl.ds(block * dests, dests)] = done.reshape(dests, rows_to, HEAD_DIM)

        @pl.when(block > 0)
        def _():
            o_copies(block - 1, lambda copy: copy.start())

        return carry

    lax.fori_loop(0, ZS * per, last, 0)
    own = core * 2 * ni + group * 4 + zl
    obuf[own] = ob[zl * ni + inner]
    o_copies(ZS * per - 1, lambda copy: copy.start())

    to_all(lambda copy: copy.wait_send())
    for kind in range(4):
        for j in range(ZS):
            for h in range(HALVES):
                x_copy(kind, j, h).wait_send()
    rest = pltpu.make_async_remote_copy(
        src_ref=obuf.at[pl.ds(0, ZS * ni - 1)], dst_ref=obuf.at[pl.ds(0, ZS * ni - 1)],
        send_sem=osend, recv_sem=orecv, device_id=at(right, zl, inner), device_id_type=MESH,
    )
    rest.wait_send()
    rest.wait_recv()
    out_ref[...] = obuf[...]


def per_device(ni, queries, keys, values):
    tok, nets, cols = queries.shape
    half = tok // HALVES

    def split(a):
        return a.reshape(tok, nets, 2, HEAD_DIM).transpose(1, 2, 0, 3)

    q = split(queries)
    k = split(keys).reshape(nets, 2, HALVES, half, HEAD_DIM)
    v = split(values).reshape(nets, 2, HALVES, half, HEAD_DIM)
    heads = 2 * ni
    rows_to = tok // ni
    vmem = pl.BlockSpec(memory_space=pltpu.VMEM)
    dma = pltpu.SemaphoreType.DMA
    out = pl.pallas_call(
        functools.partial(kernel, ni, tok),
        out_shape=jax.ShapeDtypeStruct((nets * heads, rows_to, HEAD_DIM), jnp.bfloat16),
        in_specs=[vmem] * 3,
        out_specs=vmem,
        scratch_shapes=[
            pltpu.VMEM((ZS, tok, HEAD_DIM), jnp.bfloat16),
            pltpu.VMEM((ZS, HALVES, XS, 2, half, HEAD_DIM), jnp.bfloat16),
            pltpu.VMEM((ZS * tok, 2 * HEAD_DIM), jnp.float32),
            pltpu.VMEM((ZS * tok, HEAD_DIM), jnp.float32),
            pltpu.VMEM((ZS * ni, rows_to, HEAD_DIM), jnp.bfloat16),
            pltpu.VMEM((nets * heads, rows_to, HEAD_DIM), jnp.bfloat16),
            dma((1 + 2 * HALVES, 2, 2)),
            dma((1 + 2 * HALVES, ZS)),
            dma((4, ZS, HALVES)),
            dma((4, ZS, HALVES)),
            dma,
            dma,
        ],
        compiler_params=pltpu.CompilerParams(collective_id=0, has_side_effects=True, vmem_limit_bytes=48 << 20),
        name="attend",
    )(q, k, v)
    return out.reshape(nets, heads, rows_to, HEAD_DIM).transpose(2, 0, 1, 3).reshape(rows_to, nets, heads * HEAD_DIM)


def solution(mesh):
    spec = P("outer", None, "inner")
    return jax.shard_map(
        functools.partial(per_device, mesh.shape["inner"]),
        mesh=mesh,
        in_specs=(spec, spec, spec),
        out_specs=P(("outer", "inner"), None, None),
        check_vma=False,
    )
```

time: 322 us -> 95.2 us (0.30); the launches traced: 318 us -> 95 us
  waiting for transfers between devices: 204 us -> 0 us
  Pallas kernels: 0 us -> 89.7 us
  matrix products: 30.6 us -> 0 us
  local copies, waits for them, and re-layouts: 34.4 us -> 5.22 us
  blocking collectives: 22.5 us -> 0 us
  between operations: 13.5 us -> 0.07 us
  other arithmetic: 11.9 us -> 0 us
    all_gather x2 -> x0, waiting for transfers between devices: 204 us -> none  [the longest x1 103 us: per_device(): lax.all_gather(flat_keys, 'outer', axis=0, tiled=True)]
    pallas_call x0 -> x1, Pallas kernels: none -> 89.7 us  [per_device(): pl.pallas_call(functools.partial(kernel, ni, tok), out_shape=jax.ShapeDty...]
    dot_general x32 -> x0, matrix products: 30.6 us -> none  [the longest x16 18.3 us: attend_keys(): jnp.einsum('qhk,khd->qhd', weights.astype(jnp.bfloat16), value_heads, pre...]
    dynamic_slice x48 -> x0, local copies, waits for them, and re-layouts: 27.2 us -> none  [attend_piece(): running, unused = lax.scan(one_block, running, (key_blocks, value_blocks))]
    all_to_all x1 -> x0, blocking collectives: 22.5 us -> none  [per_device(): lax.all_to_all(local_out, 'inner', split_axis=0, concat_axis=2, tiled=True)]
    reduce_sum x16 -> x0, other arithmetic: 11.3 us -> none  [attend_keys(): totals = totals * shrink + jnp.sum(weights, axis=2)]
  transfers between devices with their start and end apart: 2 -> 0, of which waited for: 2 -> 0; matrix products, arithmetic and copies ran while one was open for 1% -> 0% of each run, Pallas kernels for 0% -> 0%
where the time goes in v1:
time: 95.2 us; the launch traced here: 95 us
  Pallas kernels  89.7 us (94%)
  local copies, waits for them, and re-layouts  5.22 us (5%)
    pallas_call x1, Pallas kernels, per_device(): pl.pallas_call(functools.partial(kernel, ni, tok), out_shape=jax.ShapeDty...  89.7 us
    unnamed x5, local copies, waits for them, and re-layouts  3.03 us

profile of v1, /device:TPU:1, one launch (start us, length us, event | category | flops | bytes accessed | tf_op | source)
XLA Modules:
  0.0 95.0 jit_solution(17412623401031947346)
XLA Ops:
  0.0 1.3 %copy.7 = bf16[512,2,256]{0,2,1:T(8,128)(2,1)S(1)} copy(bf16[512,2,256]{2,1,0:T(2,128)(2,1)} %param.3) | data formatting | bytes 1048576 | tf_op args[0]
  1.3 0.0 copy-start
  1.3 0.3 copy.8
  1.6 0.8 copy-done
  2.4 0.3 reshape.22
  2.7 0.0 copy-start.1
  2.7 0.1 copy.9
  2.8 1.0 %copy-done.1 = bf16[512,2,256]{2,1,0:T(2,128)(2,1)S(1)} copy-done((bf16[512,2,256]{2,1,0:T(2,128)(2,1)S(1)}, bf16[512,2,256]{2,1,0:T(2,128)(2,1)}, u32[]{:S(2)}) %copy-start.1) | copy-done | bytes 524312
  3.7 0.3 reshape.24
  4.1 0.1 copy.10
  4.2 89.7 %attend.1 = bf16[64,32,128]{2,1,0:T(8,128)(2,1)S(1)} custom-call(bf16[2,2,512,128]{3,2,1,0:T(8,128)(2,1)S(1)} %bitcast.13, bf16[2,2,2,256,128]{4,3,2,1,0:T(8,128)(2,1)S(1)} %bitcast.14, bf16[2,2,2,256,128]{4,3,2,1,0:T(8,128)(2,1)S(1)} %bitcast.15), custom_call_target="tpu_custom_call" | custom-call | tf_op jit(solution)/shard_map/attend/pallas_call | solution.py:261
  93.9 0.2 copy.11
  94.1 0.9 reshape.27
Async XLA Ops:
  1.3 1.0 %copy-start = (bf16[512,2,256]{2,1,0:T(2,128)(2,1)S(1)}, bf16[512,2,256]{2,1,0:T(2,128)(2,1)}, u32[]{:S(2)}) copy-start(bf16[512,2,256]{2,1,0:T(2,128)(2,1)} %param.4) | copy-start | bytes 1572868
  2.7 1.0 %copy-start.1 = (bf16[512,2,256]{2,1,0:T(2,128)(2,1)S(1)}, bf16[512,2,256]{2,1,0:T(2,128)(2,1)}, u32[]{:S(2)}) copy-start(bf16[512,2,256]{2,1,0:T(2,128)(2,1)} %param.5) | copy-start | bytes 1572868

commit v2 on v0

v2 whole, which is shorter than its diff:
```python
import functools
import math

import jax
import jax.numpy as jnp
from jax import lax
from jax.experimental import pallas as pl
from jax.experimental.pallas import tpu as pltpu
from jax.sharding import PartitionSpec as P

HEAD_DIM = 128
XS = 4
ZS = 4
CUTS = 4
FACTOR = math.log2(math.e) / math.sqrt(HEAD_DIM)
MESH = pl.DeviceIdType.MESH


def kernel(
    ni, tok, q_hbm, k_hbm, v_hbm, out_ref,
    raw, qd, kvd, qb, kvb, acc, peak, ob, obuf,
    score_a, score_b, peak_a, peak_b, shrink_a, shrink_b,
    load, zsend, zrecv, xsend, xrecv, osend, orecv,
):
    piece = tok // CUTS
    rows_to = tok // ni
    keys_at = 2 * XS * piece
    outer, inner = lax.axis_index("outer"), lax.axis_index("inner")
    x, zl = outer % XS, outer // XS
    core, group = inner % 2, inner // 2
    z_hi, y = group % 2, group // 2
    right, left, far = (x + 1) % XS, (x + XS - 1) % XS, (x + 2) % XS

    def at(x_at, z_at, inner_at):
        return {"outer": z_at * XS + x_at, "inner": inner_at}

    loads = [pltpu.make_async_copy(ref, raw.at[i], load.at[i]) for i, ref in enumerate((q_hbm, k_hbm, v_hbm))]
    for copy in loads:
        copy.start()

    barrier = pltpu.get_barrier_semaphore()

    def hello(index, carry):
        z_at, inner_at = index // ni, index % ni

        @pl.when(jnp.logical_or(z_at != zl, inner_at != inner))
        def _():
            pl.semaphore_signal(barrier, inc=1, device_id=at(x, z_at, inner_at), device_id_type=MESH)

        return carry

    lax.fori_loop(0, ZS * ni, hello, 0)
    for x_at in (left, right):
        pl.semaphore_signal(barrier, inc=1, device_id=at(x_at, zl, inner), device_id_type=MESH)

    acc[...] = jnp.zeros_like(acc)
    peak[...] = jnp.full_like(peak, -1e30)

    span = min(128, piece)
    row = lax.broadcasted_iota(jnp.int32, (2 * span, 2 * span), 0)
    col = lax.broadcasted_iota(jnp.int32, (2 * span, 2 * span), 1)
    take = jnp.where(row < span, 2 * row, 2 * (row - span) + 1)
    sort = jnp.where(col == take, 1.0, 0.0).astype(jnp.bfloat16)
    for i in range(3):
        loads[i].wait()
        for s in range(tok // span):
            mixed = raw[i, s * span:(s + 1) * span].reshape(2 * span, 2 * HEAD_DIM)
            parted = jnp.dot(sort, mixed, preferred_element_type=jnp.float32).astype(jnp.bfloat16)
            for net in range(2):
                for hh in range(2):
                    part = parted[net * span:(net + 1) * span, hh * HEAD_DIM:(hh + 1) * HEAD_DIM]
                    if i == 0:
                        qd[net, hh, s * span:(s + 1) * span] = part
                    else:
                        r, off = s * span // piece, s * span % piece
                        kvd[net, hh, r, i - 1, off:off + span] = part

    keeps = zl // 2 == core
    mine, side = zl % 2, zl // 2

    @pl.when(keeps)
    def _():
        qb[zl] = qd[core, mine]
        for r in range(CUTS):
            kvb[zl, r, x] = kvd[core, mine, r]

    pl.semaphore_wait(barrier, ZS * ni - 1 + 2)

    def z_copy(what, hh, net):
        if what == 0:
            src, dst = qd.at[net, hh], qb.at[zl]
        else:
            src, dst = kvd.at[net, hh, what - 1], kvb.at[zl, what - 1, x]
        return pltpu.make_async_remote_copy(
            src_ref=src, dst_ref=dst,
            send_sem=zsend.at[what, hh, net], recv_sem=zrecv.at[what, zl],
            device_id=at(x, 2 * core + hh, group * 2 + net), device_id_type=MESH,
        )

    def to_all(act, order):
        for what in order:
            for hh in range(2):
                for net in range(2):
                    goes = jnp.logical_or(2 * core + hh != zl, net != core)

                    @pl.when(goes)
                    def _(what=what, hh=hh, net=net):
                        act(z_copy(what, hh, net))

    pl.when(keeps)(lambda: to_all(lambda copy: copy.start(), (1, 2, 0, 3, 4)))
    pl.when(jnp.logical_not(keeps))(lambda: to_all(lambda copy: copy.start(), range(1 + CUTS)))

    z_of = (zl, zl + 1 - 2 * mine, (ZS - 1) * (1 - side), 2 - side)

    def wait_for(ref, sem):
        pltpu.make_async_remote_copy(
            src_ref=ref, dst_ref=ref, send_sem=sem, recv_sem=sem,
            device_id=at(right, zl, inner), device_id_type=MESH,
        ).wait_recv()

    def z_arrived(what, j):
        z_at = z_of[j]
        ref = qb.at[z_at] if what == 0 else kvb.at[z_at, what - 1, x]
        if j == 0:
            @pl.when(jnp.logical_not(keeps))
            def _():
                wait_for(ref, zrecv.at[what, z_at])
        else:
            wait_for(ref, zrecv.at[what, z_at])

    def x_copy(kind, j, r):
        block = kvb.at[z_of[j], r]
        ref = (block.at[x], block.at[x], block.at[left, 0], block.at[right, 1])[kind]
        return pltpu.make_async_remote_copy(
            src_ref=ref, dst_ref=ref,
            send_sem=xsend.at[kind, j, r], recv_sem=xrecv.at[kind, j, r],
            device_id=at((right, left)[kind % 2], zl, inner), device_id_type=MESH,
        )

    def x_arrived(kind, j, r):
        block = kvb.at[z_of[j], r]
        ref = (block.at[left], block.at[right], block.at[far, 0], block.at[far, 1])[kind]
        wait_for(ref, xrecv.at[kind, j, r])

    def stage_a(j, r):
        z_arrived(1 + r, j)
        x_copy(0, j, r).start()
        x_copy(1, j, r).start()

    def stage_b(j, r):
        x_arrived(0, j, r)
        x_copy(2, j, r).start()
        x_arrived(1, j, r)
        x_copy(3, j, r).start()

    def stage_c(j, r):
        x_arrived(2, j, r)
        x_arrived(3, j, r)

    buffers = ((score_a, peak_a, shrink_a), (score_b, peak_b, shrink_b))

    def order(b):
        return (zl + b) % ZS

    def rows_of(b):
        return pl.ds(pl.multiple_of(order(b) * tok, tok), tok)

    def scores(z_at, first, b):
        score, top, shrink = buffers[b % 2]
        keys = kvb[z_at, pl.ds(first, 2), :, 0].reshape(keys_at, HEAD_DIM)
        s = lax.dot_general(qb[order(b)], keys, (((1,), (1,)), ((), ())), preferred_element_type=jnp.float32)
        score[...] = s
        before = peak[rows_of(b)]
        now = jnp.maximum(before, jnp.max(s, axis=1, keepdims=True) * FACTOR)
        peak[rows_of(b)] = now
        top[...] = now
        shrink[...] = jnp.exp2(before - now)

    def apply(z_at, first, b):
        score, top, shrink = buffers[b % 2]
        weights = jnp.exp2(score[...] * FACTOR - jnp.tile(top[...], (1, keys_at // HEAD_DIM)))
        values = kvb[z_at, pl.ds(first, 2), :, 1].reshape(keys_at, HEAD_DIM)
        wide = jnp.concatenate([values, jnp.ones_like(values)], axis=1)
        new = jnp.dot(weights.astype(jnp.bfloat16), wide, preferred_element_type=jnp.float32)
        return acc[rows_of(b)] * jnp.tile(shrink[...], (1, 2)) + new

    def fold(z_at, first):
        scores(z_at, first, 0)
        for b in range(ZS):
            if b + 1 < ZS:
                scores(z_at, first, b + 1)
            acc[rows_of(b)] = apply(z_at, first, b)

    def o_send(b):
        z_at = order(b)

        def one(e, carry):
            z_hi_at = jnp.where(e < ni // 2, 1 - z_hi, z_hi) if ni > 2 else z_hi
            y_at = (y + (e % (ni // 2)) // 2) % (ni // 4) if ni > 2 else y
            inner_at = (y_at * 2 + z_hi_at) * 2 + (core + e) % 2

            @pl.when(jnp.logical_or(z_at != zl, inner_at != inner))
            def _():
                pltpu.make_async_remote_copy(
                    src_ref=ob.at[z_at * ni + inner_at],
                    dst_ref=obuf.at[core * 2 * ni + group * 4 + zl],
                    send_sem=osend, recv_sem=orecv,
                    device_id=at(x, z_at, inner_at), device_id_type=MESH,
                ).start()

            return carry

        lax.fori_loop(0, ni, one, 0)

    A, B, C = stage_a, stage_b, stage_c
    for r in range(CUTS):
        A(0, r)
    B(0, 0), B(0, 1), A(1, 0), B(0, 2), A(1, 1), B(0, 3), B(1, 0)
    for j in range(ZS):
        z_arrived(0, j)

    def before0():
        B(1, 1), C(0, 0), C(0, 1)

    def before1():
        A(1, 2), A(2, 0), A(3, 0), C(0, 2), C(0, 3)

    def before2():
        A(1, 3), A(2, 1), B(1, 2), B(2, 0), B(3, 0), C(1, 0), C(1, 1)

    def before3():
        A(2, 2), B(1, 3), B(2, 1), A(2, 3), C(1, 2), C(1, 3)

    def before4():
        B(2, 2), B(2, 3), A(3, 1), C(2, 0), C(2, 1)

    def before5():
        A(3, 2), B(3, 1), A(3, 3), C(2, 2), C(2, 3)

    def before6():
        B(3, 2), B(3, 3), C(3, 0), C(3, 1)

    def chunk(t, carry):
        for step, before in enumerate((before0, before1, before2, before3, before4, before5, before6)):
            pl.when(t == step)(before)
        near, across = jnp.where(t < 2, z_of[0], z_of[1]), jnp.where(t < 6, z_of[2], z_of[3])
        fold(jnp.where(t < 4, near, across), t % 2 * 2)
        return carry

    lax.fori_loop(0, 7, chunk, 0)
    C(3, 2), C(3, 3)

    last = (z_of[3], 2)
    scores(*last, 0)
    for b in range(ZS):
        if b + 1 < ZS:
            scores(*last, b + 1)
        total = apply(*last, b)
        done = (total[:, :HEAD_DIM] / total[:, HEAD_DIM:]).astype(jnp.bfloat16)
        ob[pl.ds(order(b) * ni, ni)] = done.reshape(ni, rows_to, HEAD_DIM)
        o_send(b)
    own = core * 2 * ni + group * 4 + zl
    obuf[own] = ob[zl * ni + inner]

    to_all(lambda copy: copy.wait_send(), range(1 + CUTS))
    for kind in range(4):
        for j in range(ZS):
            for r in range(CUTS):
                x_copy(kind, j, r).wait_send()
    rest = pltpu.make_async_remote_copy(
        src_ref=obuf.at[pl.ds(0, ZS * ni - 1)], dst_ref=obuf.at[pl.ds(0, ZS * ni - 1)],
        send_sem=osend, recv_sem=orecv, device_id=at(right, zl, inner), device_id_type=MESH,
    )
    rest.wait_send()
    rest.wait_recv()
    out_ref[...] = obuf[...]


def per_device(ni, queries, keys, values):
    tok, nets, cols = queries.shape
    heads = 2 * ni
    rows_to = tok // ni
    piece = tok // CUTS
    hbm = pl.BlockSpec(memory_space=pltpu.HBM)
    dma = pltpu.SemaphoreType.DMA
    bf16, f32 = jnp.bfloat16, jnp.float32
    out = pl.pallas_call(
        functools.partial(kernel, ni, tok),
        out_shape=jax.ShapeDtypeStruct((nets * heads, rows_to, HEAD_DIM), bf16),
        in_specs=[hbm] * 3,
        out_specs=pl.BlockSpec(memory_space=pltpu.VMEM),
        scratch_shapes=[
            pltpu.VMEM((3, tok, nets, cols), bf16),
            pltpu.VMEM((nets, 2, tok, HEAD_DIM), bf16),
            pltpu.VMEM((nets, 2, CUTS, 2, piece, HEAD_DIM), bf16),
            pltpu.VMEM((ZS, tok, HEAD_DIM), bf16),
            pltpu.VMEM((ZS, CUTS, XS, 2, piece, HEAD_DIM), bf16),
            pltpu.VMEM((ZS * tok, 2 * HEAD_DIM), f32),
            pltpu.VMEM((ZS * tok, HEAD_DIM), f32),
            pltpu.VMEM((ZS * ni, rows_to, HEAD_DIM), bf16),
            pltpu.VMEM((nets * heads, rows_to, HEAD_DIM), bf16),
            pltpu.VMEM((tok, 2 * XS * piece), f32),
            pltpu.VMEM((tok, 2 * XS * piece), f32),
            pltpu.VMEM((tok, HEAD_DIM), f32),
            pltpu.VMEM((tok, HEAD_DIM), f32),
            pltpu.VMEM((tok, HEAD_DIM), f32),
            pltpu.VMEM((tok, HEAD_DIM), f32),
            dma((3,)),
            dma((1 + CUTS, 2, 2)),
            dma((1 + CUTS, ZS)),
            dma((4, ZS, CUTS)),
            dma((4, ZS, CUTS)),
            dma,
            dma,
        ],
        compiler_params=pltpu.CompilerParams(collective_id=0, has_side_effects=True, vmem_limit_bytes=56 << 20),
        name="attend",
    )(queries, keys, values)
    return out.reshape(nets, heads, rows_to, HEAD_DIM).transpose(2, 0, 1, 3).reshape(rows_to, nets, heads * HEAD_DIM)


def solution(mesh):
    spec = P("outer", None, "inner")
    return jax.shard_map(
        functools.partial(per_device, mesh.shape["inner"]),
        mesh=mesh,
        in_specs=(spec, spec, spec),
        out_specs=P(("outer", "inner"), None, None),
        check_vma=False,
    )
```

time: 322 us -> 78 us (0.24); the launches traced: 318 us -> 77.9 us
  waiting for transfers between devices: 204 us -> 0 us
  Pallas kernels: 0 us -> 75.7 us
  local copies, waits for them, and re-layouts: 34.4 us -> 2.16 us
  matrix products: 30.6 us -> 0 us
  blocking collectives: 22.5 us -> 0 us
  between operations: 13.5 us -> 0.01 us
  other arithmetic: 11.9 us -> 0 us
    all_gather x2 -> x0, waiting for transfers between devices: 204 us -> none  [the longest x1 103 us: per_device(): lax.all_gather(flat_keys, 'outer', axis=0, tiled=True)]
    pallas_call x0 -> x1, Pallas kernels: none -> 75.7 us  [per_device(): pl.pallas_call(functools.partial(kernel, ni, tok), out_shape=jax.ShapeDty...]
    dot_general x32 -> x0, matrix products: 30.6 us -> none  [the longest x16 18.3 us: attend_keys(): jnp.einsum('qhk,khd->qhd', weights.astype(jnp.bfloat16), value_heads, pre...]
    dynamic_slice x48 -> x0, local copies, waits for them, and re-layouts: 27.2 us -> none  [attend_piece(): running, unused = lax.scan(one_block, running, (key_blocks, value_blocks))]
    all_to_all x1 -> x0, blocking collectives: 22.5 us -> none  [per_device(): lax.all_to_all(local_out, 'inner', split_axis=0, concat_axis=2, tiled=True)]
    reduce_sum x16 -> x0, other arithmetic: 11.3 us -> none  [attend_keys(): totals = totals * shrink + jnp.sum(weights, axis=2)]
    unnamed x4 -> x0, local copies, waits for them, and re-layouts: 5.43 us -> none
  transfers between devices with their start and end apart: 2 -> 0, of which waited for: 2 -> 0; matrix products, arithmetic and copies ran while one was open for 1% -> 0% of each run, Pallas kernels for 0% -> 0%
where the time goes in v2:
time: 78 us; the launch traced here: 77.9 us
  Pallas kernels  75.7 us (97%)
  local copies, waits for them, and re-layouts  2.16 us (3%)
    pallas_call x1, Pallas kernels, per_device(): pl.pallas_call(functools.partial(kernel, ni, tok), out_shape=jax.ShapeDty...  75.7 us

profile of v2, /device:TPU:1, one launch (start us, length us, event | category | flops | bytes accessed | tf_op | source)
XLA Modules:
  0.0 77.9 jit_solution(2014827451597397518)
XLA Ops:
  0.0 75.7 %attend.1 = bf16[64,32,128]{2,1,0:T(8,128)(2,1)} custom-call(bf16[512,2,256]{2,1,0:T(2,128)(2,1)} %q_hbm.1, bf16[512,2,256]{2,1,0:T(2,128)(2,1)} %k_hbm.1, bf16[512,2,256]{2,1,0:T(2,128)(2,1)} %v_hbm.1), custom_call_target="tpu_custom_call" | custom-call | tf_op jit(solution)/shard_map/attend/pallas_call | solution.py:287
  75.7 1.2 %copy.4 = bf16[32,2,32,128]{3,2,1,0:T(8,128)(2,1)S(1)} copy(bf16[32,2,32,128]{3,0,2,1:T(8,128)(2,1)} %bitcast.5) | data formatting | bytes 1048576 | tf_op jit(solution)/shard_map/transpose | solution.py:319
  77.0 0.9 %reshape.7 = bf16[32,2,4096]{2,1,0:T(2,128)(2,1)} reshape(bf16[32,2,32,128]{3,2,1,0:T(8,128)(2,1)S(1)} %copy.4) | data formatting | bytes 1048576 | tf_op jit(solution)/shard_map/reshape | solution.py:319

commit v3 on v2

--- a/solution.py
+++ b/solution.py
@@ -24,7 +24,6 @@
 ):
     piece = tok // CUTS
     rows_to = tok // ni
-    keys_at = 2 * XS * piece
     outer, inner = lax.axis_index("outer"), lax.axis_index("inner")
     x, zl = outer % XS, outer // XS
     core, group = inner % 2, inner // 2
@@ -107,8 +106,15 @@
                     def _(what=what, hh=hh, net=net):
                         act(z_copy(what, hh, net))
 
-    pl.when(keeps)(lambda: to_all(lambda copy: copy.start(), (1, 2, 0, 3, 4)))
-    pl.when(jnp.logical_not(keeps))(lambda: to_all(lambda copy: copy.start(), range(1 + CUTS)))
+    across = jnp.logical_not(keeps)
+    at_end = jnp.logical_or(zl == 0, zl == ZS - 1)
+
+    def start(cond, order):
+        pl.when(cond)(lambda: to_all(lambda copy: copy.start(), order))
+
+    start(keeps, (1, 2, 0, 3, 4))
+    start(jnp.logical_and(across, at_end), (0, 1, 2, 3, 4))
+    start(jnp.logical_and(across, jnp.logical_not(at_end)), (1, 2, 3, 4, 0))
 
     z_of = (zl, zl + 1 - 2 * mine, (ZS - 1) * (1 - side), 2 - side)
 
@@ -157,17 +163,18 @@
         x_arrived(2, j, r)
         x_arrived(3, j, r)
 
+    width = 2 * XS * piece
     buffers = ((score_a, peak_a, shrink_a), (score_b, peak_b, shrink_b))
 
     def order(b):
-        return (zl + b) % ZS
+        return z_of[b]
 
     def rows_of(b):
         return pl.ds(pl.multiple_of(order(b) * tok, tok), tok)
 
-    def scores(z_at, first, b):
-        score, top, shrink = buffers[b % 2]
-        keys = kvb[z_at, pl.ds(first, 2), :, 0].reshape(keys_at, HEAD_DIM)
+    def scores(z_at, first, b, into):
+        score, top, shrink = buffers[into % 2]
+        keys = kvb[z_at, pl.ds(first, 2), :, 0].reshape(width, HEAD_DIM)
         s = lax.dot_general(qb[order(b)], keys, (((1,), (1,)), ((), ())), preferred_element_type=jnp.float32)
         score[...] = s
         before = peak[rows_of(b)]
@@ -176,91 +183,87 @@
         top[...] = now
         shrink[...] = jnp.exp2(before - now)
 
-    def apply(z_at, first, b):
-        score, top, shrink = buffers[b % 2]
-        weights = jnp.exp2(score[...] * FACTOR - jnp.tile(top[...], (1, keys_at // HEAD_DIM)))
-        values = kvb[z_at, pl.ds(first, 2), :, 1].reshape(keys_at, HEAD_DIM)
+    def apply(z_at, first, b, into):
+        score, top, shrink = buffers[into % 2]
+        weights = jnp.exp2(score[...] * FACTOR - jnp.tile(top[...], (1, width // HEAD_DIM)))
+        values = kvb[z_at, pl.ds(first, 2), :, 1].reshape(width, HEAD_DIM)
         wide = jnp.concatenate([values, jnp.ones_like(values)], axis=1)
         new = jnp.dot(weights.astype(jnp.bfloat16), wide, preferred_element_type=jnp.float32)
         return acc[rows_of(b)] * jnp.tile(shrink[...], (1, 2)) + new
 
-    def fold(z_at, first):
-        scores(z_at, first, 0)
-        for b in range(ZS):
-            if b + 1 < ZS:
-                scores(z_at, first, b + 1)
-            acc[rows_of(b)] = apply(z_at, first, b)
+    def fold(keys, between):
+        scores(*keys, 0, 0)
+        for b in range(ZS - 1):
+            between(1 + b)
+            if b + 2 < ZS:
+                scores(*keys, b + 1, b + 1)
+            acc[rows_of(b)] = apply(*keys, b, b)
+
+    slot = core * 2 * ni + group * 4 + zl
 
     def o_send(b):
         z_at = order(b)
-
-        def one(e, carry):
-            z_hi_at = jnp.where(e < ni // 2, 1 - z_hi, z_hi) if ni > 2 else z_hi
-            y_at = (y + (e % (ni // 2)) // 2) % (ni // 4) if ni > 2 else y
-            inner_at = (y_at * 2 + z_hi_at) * 2 + (core + e) % 2
-
-            @pl.when(jnp.logical_or(z_at != zl, inner_at != inner))
-            def _():
-                pltpu.make_async_remote_copy(
-                    src_ref=ob.at[z_at * ni + inner_at],
-                    dst_ref=obuf.at[core * 2 * ni + group * 4 + zl],
-                    send_sem=osend, recv_sem=orecv,
-                    device_id=at(x, z_at, inner_at), device_id_type=MESH,
-                ).start()
-
-            return carry
-
-        lax.fori_loop(0, ni, one, 0)
+        for e in range(ni):
+            z_hi_at = (1 - z_hi if e < ni // 2 else z_hi) if ni > 2 else z_hi
+            y_at = (y + 1 + (e % (ni // 2)) // 2) % (ni // 4) if ni > 2 else y
+            inner_at = (y_at * 2 + z_hi_at) * 2 + (core + 1 + e) % 2
+            if b == 0 and e == ni - 1:
+                continue
+            pltpu.make_async_remote_copy(
+                src_ref=ob.at[z_at * ni + inner_at], dst_ref=obuf.at[slot], send_sem=osend, recv_sem=orecv,
+                device_id=at(x, z_at, inner_at), device_id_type=MESH,
+            ).start()
+
+    def finish(b, total):
+        done = (total[:, :HEAD_DIM] / total[:, HEAD_DIM:]).astype(jnp.bfloat16)
+        ob[pl.ds(order(b) * ni, ni)] = done.reshape(ni, rows_to, HEAD_DIM)
+        o_send(b)
 
     A, B, C = stage_a, stage_b, stage_c
     for r in range(CUTS):
         A(0, r)
-    B(0, 0), B(0, 1), A(1, 0), B(0, 2), A(1, 1), B(0, 3), B(1, 0)
-    for j in range(ZS):
+    B(0, 0), A(1, 0), B(0, 1), A(3, 0), B(0, 2), A(1, 1), B(0, 3), B(1, 0)
+    for j in range(ZS - 1):
         z_arrived(0, j)
 
-    def before0():
-        B(1, 1), C(0, 0), C(0, 1)
-
-    def before1():
-        A(1, 2), A(2, 0), A(3, 0), C(0, 2), C(0, 3)
-
-    def before2():
-        A(1, 3), A(2, 1), B(1, 2), B(2, 0), B(3, 0), C(1, 0), C(1, 1)
-
-    def before3():
-        A(2, 2), B(1, 3), B(2, 1), A(2, 3), C(1, 2), C(1, 3)
-
-    def before4():
-        B(2, 2), B(2, 3), A(3, 1), C(2, 0), C(2, 1)
-
-    def before5():
-        A(3, 2), B(3, 1), A(3, 3), C(2, 2), C(2, 3)
-
-    def before6():
-        B(3, 2), B(3, 3), C(3, 0), C(3, 1)
-
-    def chunk(t, carry):
-        for step, before in enumerate((before0, before1, before2, before3, before4, before5, before6)):
-            pl.when(t == step)(before)
-        near, across = jnp.where(t < 2, z_of[0], z_of[1]), jnp.where(t < 6, z_of[2], z_of[3])
-        fold(jnp.where(t < 4, near, across), t % 2 * 2)
-        return carry
-
-    lax.fori_loop(0, 7, chunk, 0)
+    chunks = ((0, 0), (0, 2), (1, 0), (3, 0), (1, 2), (2, 0), (2, 2), (3, 2))
+    plan = (
+        ((C, 0, 0), (C, 0, 1)), ((B, 3, 0),), ((A, 3, 1),), ((B, 1, 1),),
+        ((C, 0, 2), (C, 0, 3)), (), ((A, 1, 2),), ((B, 3, 1),),
+        ((C, 1, 0), (C, 1, 1)), ((A, 3, 2), (A, 2, 0)), ((A, 1, 3),), ((B, 1, 2),),
+        ((C, 3, 0), (C, 3, 1)), ((A, 2, 1),), ((B, 3, 2), (B, 2, 0)), ((B, 1, 3),),
+        ((A, 2, 2), (B, 2, 1), (C, 1, 2), (C, 1, 3)), ((A, 2, 3),), ((B, 2, 2),), (),
+        ((C, 2, 0), (C, 2, 1)), ((A, 3, 3),), (), ((B, 2, 3),),
+        ((B, 3, 3), (C, 2, 2), (C, 2, 3)), (), (), (),
+    )
+
+    for t in range(7):
+        def moves(slot_at, t=t):
+            for act, j, r in plan[t * ZS + slot_at]:
+                act(j, r)
+
+        z_at, first = z_of[chunks[t][0]], chunks[t][1]
+        moves(0)
+        fold((z_at, first), moves)
+
+    late = ZS - 1
+
+    def of(step):
+        return z_of[chunks[step][0]], chunks[step][1]
+
     C(3, 2), C(3, 3)
-
-    last = (z_of[3], 2)
-    scores(*last, 0)
-    for b in range(ZS):
-        if b + 1 < ZS:
-            scores(*last, b + 1)
-        total = apply(*last, b)
-        done = (total[:, :HEAD_DIM] / total[:, HEAD_DIM:]).astype(jnp.bfloat16)
-        ob[pl.ds(order(b) * ni, ni)] = done.reshape(ni, rows_to, HEAD_DIM)
-        o_send(b)
-    own = core * 2 * ni + group * 4 + zl
-    obuf[own] = ob[zl * ni + inner]
+    scores(*of(7), 0, 0)
+    for b in range(ZS - 1):
+        if b + 2 < ZS:
+            scores(*of(7), b + 1, b + 1)
+        finish(b, apply(*of(7), b, b))
+    z_arrived(0, 3)
+    scores(*of(0), late, 0)
+    for step in range(7):
+        scores(*of(step + 1), late, step + 1)
+        acc[rows_of(late)] = apply(*of(step), late, step)
+    finish(late, apply(*of(7), late, 7))
+    obuf[slot] = ob[zl * ni + inner]
 
     to_all(lambda copy: copy.wait_send(), range(1 + CUTS))
     for kind in range(4):

time: 78 us -> 72.6 us (0.931); the launches traced: 77.9 us -> 71.6 us
  Pallas kernels: 75.7 us -> 69.5 us
    pallas_call x1, Pallas kernels: 75.7 us -> 69.5 us  [per_device(): pl.pallas_call(functools.partial(kernel, ni, tok), out_shape=jax.ShapeDty...]
where the time goes in v3:
time: 72.6 us; the launch traced here: 71.6 us
  Pallas kernels  69.5 us (96%)
  local copies, waits for them, and re-layouts  2.16 us (3%)
    pallas_call x1, Pallas kernels, per_device(): pl.pallas_call(functools.partial(kernel, ni, tok), out_shape=jax.ShapeDty...  69.5 us

profile of v3, /device:TPU:1, one launch (start us, length us, event | category | flops | bytes accessed | tf_op | source)
XLA Modules:
  0.0 71.6 jit_solution(3268966053750102141)
XLA Ops:
  0.0 69.5 %attend.1 = bf16[64,32,128]{2,1,0:T(8,128)(2,1)} custom-call(bf16[512,2,256]{2,1,0:T(2,128)(2,1)} %q_hbm.1, bf16[512,2,256]{2,1,0:T(2,128)(2,1)} %k_hbm.1, bf16[512,2,256]{2,1,0:T(2,128)(2,1)} %v_hbm.1), custom_call_target="tpu_custom_call" | custom-call | tf_op jit(solution)/shard_map/attend/pallas_call | solution.py:290
  69.5 1.2 %copy.4 = bf16[32,2,32,128]{3,2,1,0:T(8,128)(2,1)S(1)} copy(bf16[32,2,32,128]{3,0,2,1:T(8,128)(2,1)} %bitcast.5) | data formatting | bytes 1048576 | tf_op jit(solution)/shard_map/transpose | solution.py:322
  70.7 0.9 %reshape.7 = bf16[32,2,4096]{2,1,0:T(2,128)(2,1)} reshape(bf16[32,2,32,128]{3,2,1,0:T(8,128)(2,1)S(1)} %copy.4) | data formatting | bytes 1048576 | tf_op jit(solution)/shard_map/reshape | solution.py:322

commit v4 on v3

--- a/solution.py
+++ b/solution.py
@@ -191,10 +191,9 @@
         new = jnp.dot(weights.astype(jnp.bfloat16), wide, preferred_element_type=jnp.float32)
         return acc[rows_of(b)] * jnp.tile(shrink[...], (1, 2)) + new
 
-    def fold(keys, between):
+    def fold(*keys):
         scores(*keys, 0, 0)
         for b in range(ZS - 1):
-            between(1 + b)
             if b + 2 < ZS:
                 scores(*keys, b + 1, b + 1)
             acc[rows_of(b)] = apply(*keys, b, b)
@@ -227,29 +226,36 @@
         z_arrived(0, j)
 
     chunks = ((0, 0), (0, 2), (1, 0), (3, 0), (1, 2), (2, 0), (2, 2), (3, 2))
-    plan = (
-        ((C, 0, 0), (C, 0, 1)), ((B, 3, 0),), ((A, 3, 1),), ((B, 1, 1),),
-        ((C, 0, 2), (C, 0, 3)), (), ((A, 1, 2),), ((B, 3, 1),),
-        ((C, 1, 0), (C, 1, 1)), ((A, 3, 2), (A, 2, 0)), ((A, 1, 3),), ((B, 1, 2),),
-        ((C, 3, 0), (C, 3, 1)), ((A, 2, 1),), ((B, 3, 2), (B, 2, 0)), ((B, 1, 3),),
-        ((A, 2, 2), (B, 2, 1), (C, 1, 2), (C, 1, 3)), ((A, 2, 3),), ((B, 2, 2),), (),
-        ((C, 2, 0), (C, 2, 1)), ((A, 3, 3),), (), ((B, 2, 3),),
-        ((B, 3, 3), (C, 2, 2), (C, 2, 3)), (), (), (),
-    )
-
-    for t in range(7):
-        def moves(slot_at, t=t):
-            for act, j, r in plan[t * ZS + slot_at]:
-                act(j, r)
-
-        z_at, first = z_of[chunks[t][0]], chunks[t][1]
-        moves(0)
-        fold((z_at, first), moves)
-
-    late = ZS - 1
-
     def of(step):
         return z_of[chunks[step][0]], chunks[step][1]
+
+    plan = (
+        ((C, 0, 0), (C, 0, 1)),
+        ((B, 3, 0), (A, 3, 1), (B, 1, 1), (C, 0, 2), (C, 0, 3)),
+        ((A, 1, 2), (B, 3, 1), (A, 2, 0), (A, 3, 2), (C, 1, 0), (C, 1, 1)),
+        ((A, 1, 3), (A, 2, 1), (B, 1, 2), (B, 3, 2), (B, 2, 0), (A, 2, 2), (C, 3, 0), (C, 3, 1)),
+        ((B, 1, 3), (A, 2, 3), (B, 2, 1), (C, 1, 2), (A, 3, 3), (C, 1, 3)),
+        ((B, 2, 2), (C, 2, 0), (C, 2, 1), (B, 2, 3)),
+        ((B, 3, 3), (C, 2, 2), (C, 2, 3)),
+    )
+    for step in range(7):
+        for act, j, r in plan[step]:
+            act(j, r)
+        fold(*of(step))
+
+    late = ZS - 1
+
+
+    def catch_up(begin, end):
+        scores(*of(begin), late, begin)
+        for step in range(begin, end):
+            if step + 1 < end:
+                scores(*of(step + 1), late, step + 1)
+            total = apply(*of(step), late, step)
+            if step == 7:
+                finish(late, total)
+            else:
+                acc[rows_of(late)] = total
 
     C(3, 2), C(3, 3)
     scores(*of(7), 0, 0)
@@ -258,11 +264,7 @@
             scores(*of(7), b + 1, b + 1)
         finish(b, apply(*of(7), b, b))
     z_arrived(0, 3)
-    scores(*of(0), late, 0)
-    for step in range(7):
-        scores(*of(step + 1), late, step + 1)
-        acc[rows_of(late)] = apply(*of(step), late, step)
-    finish(late, apply(*of(7), late, 7))
+    catch_up(0, 8)
     obuf[slot] = ob[zl * ni + inner]
 
     to_all(lambda copy: copy.wait_send(), range(1 + CUTS))

time: 72.6 us -> 71 us (0.978); the launches traced: 71.6 us -> 70.9 us
  Pallas kernels: 69.5 us -> 68.7 us
    pallas_call x1, Pallas kernels: 69.5 us -> 68.7 us  [per_device(): pl.pallas_call(functools.partial(kernel, ni, tok), out_shape=jax.ShapeDty...]
where the time goes in v4:
time: 71 us; the launch traced here: 70.9 us
  Pallas kernels  68.7 us (97%)
  local copies, waits for them, and re-layouts  2.16 us (3%)
    pallas_call x1, Pallas kernels, per_device(): pl.pallas_call(functools.partial(kernel, ni, tok), out_shape=jax.ShapeDty...  68.7 us

profile of v4, /device:TPU:1, one launch (start us, length us, event | category | flops | bytes accessed | tf_op | source)
XLA Modules:
  0.0 70.9 jit_solution(10426558104056070095)
XLA Ops:
  0.0 68.7 %attend.1 = bf16[64,32,128]{2,1,0:T(8,128)(2,1)} custom-call(bf16[512,2,256]{2,1,0:T(2,128)(2,1)} %q_hbm.1, bf16[512,2,256]{2,1,0:T(2,128)(2,1)} %k_hbm.1, bf16[512,2,256]{2,1,0:T(2,128)(2,1)} %v_hbm.1), custom_call_target="tpu_custom_call" | custom-call | tf_op jit(solution)/shard_map/attend/pallas_call | solution.py:292
  68.7 1.2 %copy.4 = bf16[32,2,32,128]{3,2,1,0:T(8,128)(2,1)S(1)} copy(bf16[32,2,32,128]{3,0,2,1:T(8,128)(2,1)} %bitcast.5) | data formatting | bytes 1048576 | tf_op jit(solution)/shard_map/transpose | solution.py:324
  70.0 0.9 %reshape.7 = bf16[32,2,4096]{2,1,0:T(2,128)(2,1)} reshape(bf16[32,2,32,128]{3,2,1,0:T(8,128)(2,1)S(1)} %copy.4) | data formatting | bytes 1048576 | tf_op jit(solution)/shard_map/reshape | solution.py:324

commit v5 on v4

--- a/solution.py
+++ b/solution.py
@@ -318,7 +318,7 @@
             dma,
             dma,
         ],
-        compiler_params=pltpu.CompilerParams(collective_id=0, has_side_effects=True, vmem_limit_bytes=56 << 20),
+        compiler_params=pltpu.CompilerParams(collective_id=0, has_side_effects=True, vmem_limit_bytes=53 << 20),
         name="attend",
     )(queries, keys, values)
     return out.reshape(nets, heads, rows_to, HEAD_DIM).transpose(2, 0, 1, 3).reshape(rows_to, nets, heads * HEAD_DIM)

time: 71 us -> 69.1 us (0.973)
  local copies, waits for them, and re-layouts: 2.16 us -> 1.12 us
  Pallas kernels: 68.7 us -> 67.9 us
    transpose x1, local copies, waits for them, and re-layouts: 1.25 us -> 0.21 us  [per_device(): out.reshape(nets, heads, rows_to, HEAD_DIM).transpose(2, 0, 1, 3)]
    pallas_call x1, Pallas kernels: 68.7 us -> 67.9 us  [per_device(): pl.pallas_call(functools.partial(kernel, ni, tok), out_shape=jax.ShapeDty...]
where the time goes in v5:
time: 69.1 us; the launch traced here: 69 us
  Pallas kernels  67.9 us (98%)
  local copies, waits for them, and re-layouts  1.12 us (2%)
    pallas_call x1, Pallas kernels, per_device(): pl.pallas_call(functools.partial(kernel, ni, tok), out_shape=jax.ShapeDty...  67.9 us

profile of v5, /device:TPU:1, one launch (start us, length us, event | category | flops | bytes accessed | tf_op | source)
XLA Modules:
  0.0 69.0 jit_solution(14170195761164679050)
XLA Ops:
  0.0 67.9 %attend.1 = bf16[64,32,128]{2,1,0:T(8,128)(2,1)S(1)} custom-call(bf16[512,2,256]{2,1,0:T(2,128)(2,1)} %q_hbm.1, bf16[512,2,256]{2,1,0:T(2,128)(2,1)} %k_hbm.1, bf16[512,2,256]{2,1,0:T(2,128)(2,1)} %v_hbm.1), custom_call_target="tpu_custom_call" | custom-call | tf_op jit(solution)/shard_map/attend/pallas_call | solution.py:292
  67.9 0.2 copy.4
  68.1 0.9 %reshape.7 = bf16[32,2,4096]{2,1,0:T(2,128)(2,1)} reshape(bf16[32,2,32,128]{3,2,1,0:T(8,128)(2,1)S(1)} %copy.4) | data formatting | bytes 1048576 | tf_op jit(solution)/shard_map/reshape | solution.py:324
